TPU v7x, 32 devices: a whole 2x2x4 slice. The times are simulated.
32 devices in a mesh: gx: 4 (over y, x), gy: 4 (over z), gz: 2 (over core).
Axes of the slice: x: 2, y: 2, z: 4, core: 2. Of those that a mesh axis runs over, the one named last changes fastest.
Arguments:
- ref_image: bfloat16 [1024, 64, 256], P('gx', 'gy', 'gz'), may hold values from -6 to 6
- def_image: bfloat16 [1024, 64, 256], P('gx', 'gy', 'gz'), may hold values from -6 to 6
- displacement: float32 [3, 128, 8, 32], P(None, 'gx', 'gy', 'gz'), may hold values from -3 to 3
Outputs:
- new_displacement: float32 [3, 128, 8, 32], P(None, 'gx', 'gy', 'gz')
- fine_residual: bfloat16 [1024, 64, 256], P('gx', 'gy', 'gz')
All inputs are finite; a program needn't handle non-finite values.
Results may differ from a plain program's by a relative error of at most 0.0022.
Values may be sent and summed in bfloat16 or wider, within the bound.
A program may use at most 64 MiB of HBM per device.

v0:
```python
import jax
import jax.numpy as jnp
from jax import lax
from jax.sharding import PartitionSpec as P

stiffness = 64.0


def padded_2(cells, sides, width):
    for axis, dim in sides:
        count = lax.axis_size(axis)
        ends = count - 1
        head = lax.slice_in_dim(cells, 0, width, axis=dim)
        tail = lax.slice_in_dim(cells, cells.shape[dim] - width, cells.shape[dim], axis=dim)
        cells = jnp.concatenate(
            [
                lax.ppermute(tail, axis, [(i, (i + 1) % count) for i in range(ends)]),
                cells,
                lax.ppermute(head, axis, [((i + 1) % count, i) for i in range(ends)]),
            ],
            axis=dim,
        )
    return cells


def bin_level(image, summer):
    sizex, sizey, sizez = image.shape
    along_z = jnp.dot(
        image.reshape(sizex * sizey, sizez), summer, preferred_element_type=jnp.float32
    )
    return along_z.reshape(sizex // 8, 8, sizey // 8, 8, sizez // 8).sum((1, 3)) / 32.0


def central(padded):
    slope_x = (padded[2:, 1:-1, 1:-1] - padded[:-2, 1:-1, 1:-1]) / 2.0
    slope_y = (padded[1:-1, 2:, 1:-1] - padded[1:-1, :-2, 1:-1]) / 2.0
    slope_z = (padded[1:-1, 1:-1, 2:] - padded[1:-1, 1:-1, :-2]) / 2.0
    return (slope_x, slope_y, slope_z)


def line_matrix(count):
    return jnp.eye(count, dtype=jnp.float32) * (1.0 + 2.0 * stiffness) - stiffness * (
        jnp.eye(count, k=1, dtype=jnp.float32) + jnp.eye(count, k=-1, dtype=jnp.float32)
    )


def prolong_table(fine_count, coarse_count):
    index = jnp.arange(fine_count)
    center = index // 8 + 1
    offset = ((index % 8).astype(jnp.float32) + 0.5) / 8.0 - 0.5
    column = jnp.arange(coarse_count + 2)[None, :]
    weight = jnp.where(column == center[:, None], 1.0 - jnp.abs(offset)[:, None], 0.0)
    weight = weight + jnp.where(
        (offset[:, None] >= 0.0) & (column == center[:, None] + 1), offset[:, None], 0.0
    )
    weight = weight + jnp.where(
        (offset[:, None] < 0.0) & (column == center[:, None] - 1), -offset[:, None], 0.0
    )
    return weight


def line_solve(factor, rhs):
    items, lines, rest = rhs.shape
    flat = jnp.moveaxis(rhs, 1, 0).reshape(lines, items * rest)
    solved = jax.scipy.linalg.cho_solve((factor, True), flat)
    return jnp.moveaxis(solved.reshape(lines, items, rest), 0, 1)


def on_device(ref_image, def_image, displacement):
    sizex, sizey, sizez = ref_image.shape
    cells_x, cells_y, cells_z = (sizex // 8, sizey // 8, sizez // 8)
    summer = (jnp.arange(sizez)[:, None] // 8 == jnp.arange(cells_z)[None, :]).astype(jnp.bfloat16)
    coarse_ref = bin_level(ref_image, summer)
    coarse_def = bin_level(def_image, summer)
    ref_padded = padded_2(coarse_ref, (("gx", 0), ("gy", 1), ("gz", 2)), 1)
    slopes = central(ref_padded)
    mismatch = (
        coarse_def
        - coarse_ref
        - (slopes[0] * displacement[0] + slopes[1] * displacement[1] + slopes[2] * displacement[2])
    )
    rhs = jnp.stack([slope * mismatch for slope in slopes]).reshape(3, cells_x, cells_y * cells_z)
    lines = cells_x * lax.axis_size("gx")
    factor = jnp.linalg.cholesky(line_matrix(lines))
    whole = lax.all_gather(rhs, "gx", axis=1, tiled=True)
    solved = line_solve(factor, whole)
    step = lax.dynamic_slice_in_dim(solved, lax.axis_index("gx") * cells_x, cells_x, 1)
    new_displacement = displacement + step.reshape(3, cells_x, cells_y, cells_z)
    padded = padded_2(new_displacement, (("gx", 1), ("gy", 2), ("gz", 3)), 1)
    table_x = prolong_table(sizex, cells_x)
    table_y = prolong_table(sizey, cells_y)
    table_z = prolong_table(sizez, cells_z)
    field = jnp.einsum("ia,nabc->nibc", table_x, padded, precision=lax.Precision.HIGHEST)
    field = jnp.einsum("jb,nibc->nijc", table_y, field, precision=lax.Precision.HIGHEST)
    field = jnp.einsum("nijc,kc->nijk", field, table_z, precision=lax.Precision.HIGHEST)
    fine_padded = padded_2(ref_image, (("gx", 0), ("gy", 1), ("gz", 2)), 1)
    grads = central(fine_padded.astype(jnp.float32))
    total = def_image.astype(jnp.float32) - ref_image.astype(jnp.float32)
    total = total - grads[0] * field[0] - grads[1] * field[1] - grads[2] * field[2]
    return (new_displacement, total.astype(jnp.bfloat16))


def solution(mesh):
    return jax.shard_map(
        on_device,
        mesh=mesh,
        in_specs=(P("gx", "gy", "gz"), P("gx", "gy", "gz"), P(None, "gx", "gy", "gz")),
        out_specs=(P(None, "gx", "gy", "gz"), P("gx", "gy", "gz")),
        check_vma=False,
    )
```

profile of v0, /device:TPU:0, one launch (start us, length us, event | category | flops | bytes accessed | tf_op | source)
XLA Modules:
  0.0 144.3 jit_solution(2036556748247106592)
XLA Ops:
  0.6 1.6 %copy.116 = bf16[256,16,128]{2,0,1:T(8,128)(2,1)S(1)} copy(bf16[256,16,128]{2,1,0:T(8,128)(2,1)} %param.3) | data formatting | bytes 2097152 | tf_op args[0]
  2.3 4.9 %collective-permute-start.6 = (bf16[1,16,128]{2,0,1:T(2,128)(2,1)S(1)}, bf16[1,16,128]{2,0,1:T(2,128)(2,1)S(1)}, u32[]{:S(2)}, u32[]{:S(2)}) collective-permute-start(bf16[1,16,128]{2,0,1:T(2,128)(2,1)S(1)} %get-tuple-element.20), channel_id=1, source_target_pairs={{0,8},{8,16},{16,24},{1,9},{9,17},{17,25},{2,10},{10,18},{18,26},{... | collective-permute-start | bytes 12296 | tf_op jit(solution)/shard_map/ppermute | solution.py:17
  7.1 1.3 collective-permute-start.7
  8.9 2.0 %copy.107 = f32[4096,16]{1,0:T(8,128)} copy(f32[4096,16]{0,1:T(8,128)S(1)} %convolution_bitcast_fusion.1) | data formatting | bytes 524288 | tf_op jit(solution)/shard_map/dot_general | solution.py:28
  10.9 1.8 %reduce_sum.18 = f32[32,2,16]{2,1,0:T(2,128)S(1)} reduce(f32[32,8,2,8,16]{4,3,2,1,0:T(8,128)} %bitcast.100, f32[]{:T(128)} %constant.191.clone.1), dimensions={1,3}, to_apply=%region_2.3 | reduce | flops 64512 | bytes 266244 | tf_op jit(solution)/shard_map/reduce_sum | solution.py:31
  12.9 1.3 collective-permute-start
  14.2 5.2 %collective-permute-start.1 = (f32[1,2,16]{0,2,1:T(8,128)S(1)}, f32[1,2,16]{0,2,1:T(8,128)S(1)}, u32[]{:S(2)}, u32[]{:S(2)}) collective-permute-start(f32[1,2,16]{0,2,1:T(8,128)S(1)} %get-tuple-element.33), channel_id=1, source_target_pairs={{0,8},{8,16},{16,24},{1,9},{9,17},{17,25},{2,10},{10,18},{18,26},{... | collective-permute-start | bytes 392 | tf_op jit(solution)/shard_map/ppermute | solution.py:17
  19.9 0.6 fusion.117
  20.5 0.6 broadcast_compare_fusion.4
  21.1 0.6 broadcast_compare_fusion.2
  22.2 0.6 broadcast_compare_fusion
  22.7 0.6 fusion.116
  24.0 11.7 %cholesky.16 = f32[128,128]{1,0:T(8,128)S(1)} custom-call(f32[128,128]{1,0:T(8,128)S(1)} %add_multiply_fusion), custom_call_target="Cholesky" | custom-call | tf_op jit(solution)/shard_map/jit(cholesky)/cholesky | solution.py:84
  35.7 0.6 compare_reduce_fusion
  36.4 1.3 fusion.26
  38.1 0.6 and_select_fusion.2
  38.8 3.5 %collective-permute-start.3 = (f32[34,1,16]{0,2,1:T(8,128)S(1)}, f32[34,1,16]{0,2,1:T(8,128)S(1)}, u32[]{:S(2)}, u32[]{:S(2)}) collective-permute-start(f32[34,1,16]{0,2,1:T(8,128)S(1)} %get-tuple-element.30), channel_id=1, source_target_pairs={{0,2},{2,4},{4,6},{1,3},{3,5},{5,7},{8,10},{10,12},{12,14},{9,11},... | collective-permute-start | bytes 6536 | tf_op jit(solution)/shard_map/ppermute | solution.py:17
  42.3 1.3 collective-permute-start.2
  44.1 3.7 %collective-permute-done.2 = f32[34,1,16]{0,2,1:T(8,128)S(1)} collective-permute-done((f32[34,1,16]{0,2,1:T(8,128)S(1)}, f32[34,1,16]{0,2,1:T(8,128)S(1)}, u32[]{:S(2)}, u32[]{:S(2)}) %collective-permute-start.2) | collective-permute-done | bytes 2208 | tf_op jit(solution)/shard_map/ppermute | solution.py:19
  47.9 1.3 collective-permute-start.4
  49.2 3.0 %collective-permute-start.5 = (f32[34,4,1]{0,2,1:T(1,128)S(1)}, f32[34,4,1]{0,2,1:T(1,128)S(1)}, u32[]{:S(2)}, u32[]{:S(2)}) collective-permute-start(f32[34,4,1]{0,2,1:T(1,128)S(1)} %get-tuple-element.25), channel_id=1, source_target_pairs={{0,1},{2,3},{4,5},{6,7},{8,9},{10,11},{12,13},{14,15},{16,17},{18,... | collective-permute-start | bytes 1640 | tf_op jit(solution)/shard_map/ppermute | solution.py:17
  52.2 10.6 %custom-call.10 = f32[1,128,128]{1,2,0:T(8,128)S(1)} custom-call(f32[1,128,128]{2,1,0:T(8,128)} %fusion.26), custom_call_target="InvertDiagBlocksLowerTriangular" | custom-call | tf_op jit(solution)/shard_map/jit(_cho_solve)/triangular_solve | solution.py:65
  62.9 2.0 %copy.109 = f32[4096,16]{1,0:T(8,128)} copy(f32[4096,16]{0,1:T(8,128)S(1)} %convolution_bitcast_fusion) | data formatting | bytes 524288 | tf_op jit(solution)/shard_map/dot_general | solution.py:28
  64.9 1.8 %reduce_sum.19 = f32[32,2,16]{2,1,0:T(2,128)S(1)} reduce(f32[32,8,2,8,16]{4,3,2,1,0:T(8,128)} %bitcast.99, f32[]{:T(128)} %constant.191.clone.1), dimensions={1,3}, to_apply=%region_3.4 | reduce | flops 64512 | bytes 266244 | tf_op jit(solution)/shard_map/reduce_sum | solution.py:31
  67.3 10.8 %all_gather.3 = f32[3,128,32]{2,0,1:T(4,128)S(1)} all-gather(f32[3,32,32]{2,0,1:T(4,128)S(1)} %copy.111), channel_id=1, replica_groups=mesh['gx'=4,'gy'=4,'gz'=2] {'gx'}, dimensions={1}, use_global_device_ids=true | all-gather | bytes 61440 | tf_op jit(solution)/shard_map/all_gather | solution.py:85
  78.9 1.6 %collective-permute-start.12 = (f32[3,1,2,16]{1,3,2,0:T(8,128)S(1)}, f32[3,1,2,16]{1,3,2,0:T(8,128)S(1)}, u32[]{:S(2)}, u32[]{:S(2)}) collective-permute-start(f32[3,1,2,16]{1,3,2,0:T(8,128)S(1)} %get-tuple-element.28), channel_id=1, source_target_pairs={{0,8},{8,16},{16,24},{1,9},{9,17},{17,25},{2,10},{10,18},{18,26},{... | collective-permute-start | bytes 1160 | tf_op jit(solution)/shard_map/ppermute | solution.py:17
  80.5 1.3 collective-permute-start.13
  82.3 4.2 %collective-permute-done.13 = f32[3,1,2,16]{1,3,2,0:T(8,128)S(1)} collective-permute-done((f32[3,1,2,16]{1,3,2,0:T(8,128)S(1)}, f32[3,1,2,16]{1,3,2,0:T(8,128)S(1)}, u32[]{:S(2)}, u32[]{:S(2)}) %collective-permute-start.13) | collective-permute-done | bytes 416 | tf_op jit(solution)/shard_map/ppermute | solution.py:19
  86.6 3.5 %collective-permute-start.14 = (f32[3,34,1,16]{1,3,2,0:T(8,128)S(1)}, f32[3,34,1,16]{1,3,2,0:T(8,128)S(1)}, u32[]{:S(2)}, u32[]{:S(2)}) collective-permute-start(f32[3,34,1,16]{1,3,2,0:T(8,128)S(1)} %get-tuple-element.26), channel_id=1, source_target_pairs={{0,2},{2,4},{4,6},{1,3},{3,5},{5,7},{8,10},{10,12},{12,14},{9,11},... | collective-permute-start | bytes 19592 | tf_op jit(solution)/shard_map/ppermute | solution.py:17
  90.1 1.3 collective-permute-start.15
  91.6 4.2 %collective-permute-done.15 = f32[3,34,1,16]{1,3,2,0:T(8,128)S(1)} collective-permute-done((f32[3,34,1,16]{1,3,2,0:T(8,128)S(1)}, f32[3,34,1,16]{1,3,2,0:T(8,128)S(1)}, u32[]{:S(2)}, u32[]{:S(2)}) %collective-permute-start.15) | collective-permute-done | bytes 6560 | tf_op jit(solution)/shard_map/ppermute | solution.py:19
  95.9 1.3 collective-permute-start.16
  97.2 1.3 collective-permute-start.17
  98.6 3.5 %collective-permute-start.8 = (bf16[258,1,128]{2,0,1:T(8,128)(2,1)S(1)}, bf16[258,1,128]{2,0,1:T(8,128)(2,1)S(1)}, u32[]{:S(2)}, u32[]{:S(2)}) collective-permute-start(bf16[258,1,128]{2,0,1:T(8,128)(2,1)S(1)} %get-tuple-element.18), channel_id=1, source_target_pairs={{0,2},{2,4},{4,6},{1,3},{3,5},{5,7},{8,10},{10,12},{12,14},{9,11},... | collective-permute-start | bytes 198152 | tf_op jit(solution)/shard_map/ppermute | solution.py:17
  102.1 1.5 %collective-permute-start.9 = (bf16[258,1,128]{2,0,1:T(8,128)(2,1)S(1)}, bf16[258,1,128]{2,0,1:T(8,128)(2,1)S(1)}, u32[]{:S(2)}, u32[]{:S(2)}) collective-permute-start(bf16[258,1,128]{2,0,1:T(8,128)(2,1)S(1)} %get-tuple-element.19), channel_id=1, source_target_pairs={{2,0},{4,2},{6,4},{3,1},{5,3},{7,5},{10,8},{12,10},{14,12},{11,9},... | collective-permute-start | bytes 198152 | tf_op jit(solution)/shard_map/ppermute | solution.py:19
  104.1 1.5 %convolution_bitcast_fusion.2 = f32[3,256,16,18]{1,2,3,0:T(8,128)S(1)} fusion(f32[3,256,4,18]{1,3,2,0:T(8,128)S(1)} %convolution_bitcast_fusion.3, f32[16]{0:T(128)} %fusion.120, s32[16]{0:T(128)} %get-tuple-element.42, f32[16]{0:T(128)} %get-tuple-element.44, s32[16]{0:T(128)} %get-tuple-element.43, f32[16]{0:T(128)} %get-tuple-element.45, ...), kind=kOutput, calls=%fused_computation.19 | convolution fusion | flops 10617472 | bytes 1106336 | tf_op jit(solution)/shard_map/jb,nibc->nijc/dot_general | solution.py:94
  105.6 3.2 %collective-permute-done.9 = bf16[258,1,128]{2,0,1:T(8,128)(2,1)S(1)} collective-permute-done((bf16[258,1,128]{2,0,1:T(8,128)(2,1)S(1)}, bf16[258,1,128]{2,0,1:T(8,128)(2,1)S(1)}, u32[]{:S(2)}, u32[]{:S(2)}) %collective-permute-start.9) | collective-permute-done | bytes 66080 | tf_op jit(solution)/shard_map/ppermute | solution.py:19
  109.2 1.9 %fusion.128 = (bf16[258,18,1]{2,0,1:T(8,128)(2,1)}, bf16[258,18,1]{2,0,1:T(8,128)(2,1)}) fusion(bf16[258,18,128]{2,0,1:T(8,128)(2,1)S(1)} %pad_maximum_fusion), kind=kLoop, calls=%fused_computation.223 | loop fusion | bytes 37152 | tf_op jit(solution)/shard_map/slice | solution.py:14
  111.1 2.1 %copy.120 = bf16[258,18,1]{0,1,2:T(8,128)(2,1)S(1)} copy(bf16[258,18,1]{2,0,1:T(8,128)(2,1)} %get-tuple-element.16) | data formatting | bytes 18576 | tf_op jit(solution)/shard_map/slice | solution.py:14
  113.1 2.1 %copy.121 = bf16[258,18,1]{0,1,2:T(8,128)(2,1)S(1)} copy(bf16[258,18,1]{2,0,1:T(8,128)(2,1)} %get-tuple-element.17) | data formatting | bytes 18576 | tf_op jit(solution)/shard_map/slice | solution.py:13
  115.2 1.3 collective-permute-start.11
  116.5 3.0 %collective-permute-start.10 = (bf16[258,18,1]{0,1,2:T(8,128)(2,1)S(1)}, bf16[258,18,1]{0,1,2:T(8,128)(2,1)S(1)}, u32[]{:S(2)}, u32[]{:S(2)}) collective-permute-start(bf16[258,18,1]{0,1,2:T(8,128)(2,1)S(1)} %copy.120), channel_id=1, source_target_pairs={{0,1},{2,3},{4,5},{6,7},{8,9},{10,11},{12,13},{14,15},{16,17},{18,... | collective-permute-start | bytes 27872 | tf_op jit(solution)/shard_map/ppermute | solution.py:17
  119.6 12.0 %fusion.10 = f32[3,256,16,128]{3,1,2,0:T(8,128)} fusion(f32[3,256,16,18]{1,2,3,0:T(8,128)S(1)} %convolution_bitcast_fusion.2, f32[128]{0:T(128)S(1)} %copy-done.13, s32[128]{0:T(128)S(1)} %and_select_fusion.5, f32[128]{0:T(128)S(1)} %copy-done.9, s32[128]{0:T(128)S(1)} %copy-done.7, f32[128]{0:T(128)S(1)} %copy-done.10, s32[128]{0:T(128)S(1)} %copy-done.8, ...), kind=kOutput, calls=%fused_computation.21 | convolution fusion | flops 339761664 | bytes 7179520 | tf_op jit(solution)/shard_map/nijc,kc->nijk/dot_general | solution.py:95
  131.6 0.6 copy.122
  132.1 1.5 %copy.123 = bf16[258,18,1]{2,0,1:T(8,128)(2,1)} copy(bf16[258,18,1]{0,1,2:T(8,128)(2,1)S(1)} %collective-permute-done.11) | data formatting | bytes 18576 | tf_op jit(solution)/shard_map/ppermute | solution.py:19
  133.7 4.6 %maximum_convert_fusion = f32[258,18,130]{2,0,1:T(8,128)S(1)} fusion(bf16[258,18,1]{2,0,1:T(8,128)(2,1)} %copy.123, bf16[258,1,128]{2,0,1:T(8,128)(2,1)S(1)} %collective-permute-done.9, bf16[1,16,128]{2,0,1:T(2,128)(2,1)S(1)} %collective-permute-done.7, bf16[256,16,128]{2,0,1:T(8,128)(2,1)S(1)} %copy.116, bf16[1,16,128]{2,0,1:T(2,128)(2,1)S(1)} %collective-permute-done.6, ...), kind=kLoop, calls=%fused_computation.2 | loop fusion | flops 8452080 | bytes 3622320 | tf_op jit(solution)/shard_map/convert_element_type | solution.py:97
  138.3 4.3 %fusion.2 = bf16[256,16,128]{2,0,1:T(8,128)(2,1)S(1)} fusion(f32[3,256,16,128]{3,1,2,0:T(8,128)S(1)} %copy-done, f32[258,18,130]{2,0,1:T(8,128)S(1)} %maximum_convert_fusion, bf16[256,16,128]{2,1,0:T(8,128)(2,1)S(1)} %copy-done.3, bf16[256,16,128]{2,1,0:T(8,128)(2,1)S(1)} %copy-done.1), kind=kLoop, calls=%fused_computation.6 | loop fusion | flops 8388608 | bytes 22020096 | tf_op jit(solution)/shard_map/convert_element_type | solution.py:100
  142.6 1.6 %copy.126 = bf16[256,16,128]{2,1,0:T(8,128)(2,1)} copy(bf16[256,16,128]{2,0,1:T(8,128)(2,1)S(1)} %fusion.2) | data formatting | bytes 2097152
  (90 shorter events, 6.7 us)
Async XLA Ops:
  0.6 7.8 %copy-start.1 = (bf16[256,16,128]{2,1,0:T(8,128)(2,1)S(1)}, bf16[256,16,128]{2,1,0:T(8,128)(2,1)}, u32[]{:S(2)}) copy-start(bf16[256,16,128]{2,1,0:T(8,128)(2,1)} %param.3) | copy-start | bytes 3145732
  2.3 96.3 %collective-permute-start.6 = (bf16[1,16,128]{2,0,1:T(2,128)(2,1)S(1)}, bf16[1,16,128]{2,0,1:T(2,128)(2,1)S(1)}, u32[]{:S(2)}, u32[]{:S(2)}) collective-permute-start(bf16[1,16,128]{2,0,1:T(2,128)(2,1)S(1)} %get-tuple-element.20), channel_id=1, source_target_pairs={{0,8},{8,16},{16,24},{1,9},{9,17},{17,25},{2,10},{10,18},{18,26},{... | collective-permute-start | bytes 12296 | tf_op jit(solution)/shard_map/ppermute | solution.py:17
  7.1 91.4 %collective-permute-start.7 = (bf16[1,16,128]{2,0,1:T(2,128)(2,1)S(1)}, bf16[1,16,128]{2,0,1:T(2,128)(2,1)S(1)}, u32[]{:S(2)}, u32[]{:S(2)}) collective-permute-start(bf16[1,16,128]{2,0,1:T(2,128)(2,1)S(1)} %get-tuple-element.21), channel_id=1, source_target_pairs={{8,0},{16,8},{24,16},{9,1},{17,9},{25,17},{10,2},{18,10},{26,18},{... | collective-permute-start | bytes 12296 | tf_op jit(solution)/shard_map/ppermute | solution.py:19
  8.9 28.8 %copy-start.2 = (bf16[256,16,128]{2,1,0:T(8,128)(2,1)S(1)}, bf16[256,16,128]{2,1,0:T(8,128)(2,1)}, u32[]{:S(2)}) copy-start(bf16[256,16,128]{2,1,0:T(8,128)(2,1)} %param.4) | copy-start | bytes 3145732
  12.9 25.8 %collective-permute-start = (f32[1,2,16]{0,2,1:T(8,128)S(1)}, f32[1,2,16]{0,2,1:T(8,128)S(1)}, u32[]{:S(2)}, u32[]{:S(2)}) collective-permute-start(f32[1,2,16]{0,2,1:T(8,128)S(1)} %get-tuple-element.32), channel_id=1, source_target_pairs={{8,0},{16,8},{24,16},{9,1},{17,9},{25,17},{10,2},{18,10},{26,18},{... | collective-permute-start | bytes 392 | tf_op jit(solution)/shard_map/ppermute | solution.py:19
  14.2 24.5 %collective-permute-start.1 = (f32[1,2,16]{0,2,1:T(8,128)S(1)}, f32[1,2,16]{0,2,1:T(8,128)S(1)}, u32[]{:S(2)}, u32[]{:S(2)}) collective-permute-start(f32[1,2,16]{0,2,1:T(8,128)S(1)} %get-tuple-element.33), channel_id=1, source_target_pairs={{0,8},{8,16},{16,24},{1,9},{9,17},{17,25},{2,10},{10,18},{18,26},{... | collective-permute-start | bytes 392 | tf_op jit(solution)/shard_map/ppermute | solution.py:17
  38.8 5.3 %collective-permute-start.3 = (f32[34,1,16]{0,2,1:T(8,128)S(1)}, f32[34,1,16]{0,2,1:T(8,128)S(1)}, u32[]{:S(2)}, u32[]{:S(2)}) collective-permute-start(f32[34,1,16]{0,2,1:T(8,128)S(1)} %get-tuple-element.30), channel_id=1, source_target_pairs={{0,2},{2,4},{4,6},{1,3},{3,5},{5,7},{8,10},{10,12},{12,14},{9,11},... | collective-permute-start | bytes 6536 | tf_op jit(solution)/shard_map/ppermute | solution.py:17
  42.3 5.5 %collective-permute-start.2 = (f32[34,1,16]{0,2,1:T(8,128)S(1)}, f32[34,1,16]{0,2,1:T(8,128)S(1)}, u32[]{:S(2)}, u32[]{:S(2)}) collective-permute-start(f32[34,1,16]{0,2,1:T(8,128)S(1)} %get-tuple-element.31), channel_id=1, source_target_pairs={{2,0},{4,2},{6,4},{3,1},{5,3},{7,5},{10,8},{12,10},{14,12},{11,9},... | collective-permute-start | bytes 6536 | tf_op jit(solution)/shard_map/ppermute | solution.py:19
  47.9 18.9 %collective-permute-start.4 = (f32[34,4,1]{0,2,1:T(1,128)S(1)}, f32[34,4,1]{0,2,1:T(1,128)S(1)}, u32[]{:S(2)}, u32[]{:S(2)}) collective-permute-start(f32[34,4,1]{0,2,1:T(1,128)S(1)} %get-tuple-element.24), channel_id=1, source_target_pairs={{1,0},{3,2},{5,4},{7,6},{9,8},{11,10},{13,12},{15,14},{17,16},{19,... | collective-permute-start | bytes 1640 | tf_op jit(solution)/shard_map/ppermute | solution.py:19
  49.2 17.6 %collective-permute-start.5 = (f32[34,4,1]{0,2,1:T(1,128)S(1)}, f32[34,4,1]{0,2,1:T(1,128)S(1)}, u32[]{:S(2)}, u32[]{:S(2)}) collective-permute-start(f32[34,4,1]{0,2,1:T(1,128)S(1)} %get-tuple-element.25), channel_id=1, source_target_pairs={{0,1},{2,3},{4,5},{6,7},{8,9},{10,11},{12,13},{14,15},{16,17},{18,... | collective-permute-start | bytes 1640 | tf_op jit(solution)/shard_map/ppermute | solution.py:17
  62.9 4.0 %copy-start.5 = (f32[3,32,2,16]{1,3,2,0:T(8,128)S(1)}, f32[3,32,2,16]{1,3,2,0:T(8,128)}, u32[]{:S(2)}) copy-start(f32[3,32,2,16]{1,3,2,0:T(8,128)} %param.5) | copy-start | bytes 36868
  66.7 36.9 %copy-start.14 = (s32[256]{0:T(256)S(1)}, s32[256]{0:T(256)}, u32[]{:S(2)}) copy-start(s32[256]{0:T(256)} %broadcast_add_fusion.1) | copy-start | bytes 3076
  66.7 36.9 %copy-start.15 = (f32[256]{0:T(256)S(1)}, f32[256]{0:T(256)}, u32[]{:S(2)}) copy-start(f32[256]{0:T(256)} %fusion.117) | copy-start | bytes 3076
  66.7 36.9 %copy-start.16 = (pred[256]{0:T(512)(128)(4,1)S(1)}, pred[256]{0:T(512)(128)(4,1)}, u32[]{:S(2)}) copy-start(pred[256]{0:T(512)(128)(4,1)} %get-tuple-element.40) | copy-start | bytes 772
  66.7 36.9 %copy-start.17 = (pred[256]{0:T(512)(128)(4,1)S(1)}, pred[256]{0:T(512)(128)(4,1)}, u32[]{:S(2)}) copy-start(pred[256]{0:T(512)(128)(4,1)} %get-tuple-element.41) | copy-start | bytes 772
  67.2 36.9 %copy-start.11 = (pred[16]{0:T(512)(128)(4,1)S(1)}, pred[16]{0:T(512)(128)(4,1)}, u32[]{:S(2)}) copy-start(pred[16]{0:T(512)(128)(4,1)} %get-tuple-element.46) | copy-start | bytes 52
  67.2 36.9 %copy-start.12 = (pred[16]{0:T(512)(128)(4,1)S(1)}, pred[16]{0:T(512)(128)(4,1)}, u32[]{:S(2)}) copy-start(pred[16]{0:T(512)(128)(4,1)} %get-tuple-element.47) | copy-start | bytes 52
  78.8 30.3 %copy-start.4 = (f32[3,32,2,16]{1,3,2,0:T(8,128)}, f32[3,32,2,16]{1,3,2,0:T(8,128)S(1)}, u32[]{:S(2)}) copy-start(f32[3,32,2,16]{1,3,2,0:T(8,128)S(1)} %add.376) | copy-start | bytes 36868
  78.9 3.4 %collective-permute-start.12 = (f32[3,1,2,16]{1,3,2,0:T(8,128)S(1)}, f32[3,1,2,16]{1,3,2,0:T(8,128)S(1)}, u32[]{:S(2)}, u32[]{:S(2)}) collective-permute-start(f32[3,1,2,16]{1,3,2,0:T(8,128)S(1)} %get-tuple-element.28), channel_id=1, source_target_pairs={{0,8},{8,16},{16,24},{1,9},{9,17},{17,25},{2,10},{10,18},{18,26},{... | collective-permute-start | bytes 1160 | tf_op jit(solution)/shard_map/ppermute | solution.py:17
  80.5 6.0 %collective-permute-start.13 = (f32[3,1,2,16]{1,3,2,0:T(8,128)S(1)}, f32[3,1,2,16]{1,3,2,0:T(8,128)S(1)}, u32[]{:S(2)}, u32[]{:S(2)}) collective-permute-start(f32[3,1,2,16]{1,3,2,0:T(8,128)S(1)} %get-tuple-element.29), channel_id=1, source_target_pairs={{8,0},{16,8},{24,16},{9,1},{17,9},{25,17},{10,2},{18,10},{26,18},{... | collective-permute-start | bytes 1160 | tf_op jit(solution)/shard_map/ppermute | solution.py:19
  86.6 5.0 %collective-permute-start.14 = (f32[3,34,1,16]{1,3,2,0:T(8,128)S(1)}, f32[3,34,1,16]{1,3,2,0:T(8,128)S(1)}, u32[]{:S(2)}, u32[]{:S(2)}) collective-permute-start(f32[3,34,1,16]{1,3,2,0:T(8,128)S(1)} %get-tuple-element.26), channel_id=1, source_target_pairs={{0,2},{2,4},{4,6},{1,3},{3,5},{5,7},{8,10},{10,12},{12,14},{9,11},... | collective-permute-start | bytes 19592 | tf_op jit(solution)/shard_map/ppermute | solution.py:17
  90.1 5.7 %collective-permute-start.15 = (f32[3,34,1,16]{1,3,2,0:T(8,128)S(1)}, f32[3,34,1,16]{1,3,2,0:T(8,128)S(1)}, u32[]{:S(2)}, u32[]{:S(2)}) collective-permute-start(f32[3,34,1,16]{1,3,2,0:T(8,128)S(1)} %get-tuple-element.27), channel_id=1, source_target_pairs={{2,0},{4,2},{6,4},{3,1},{5,3},{7,5},{10,8},{12,10},{14,12},{11,9},... | collective-permute-start | bytes 19592 | tf_op jit(solution)/shard_map/ppermute | solution.py:19
  95.9 7.6 %collective-permute-start.16 = (f32[3,34,4,1]{1,3,2,0:T(1,128)S(1)}, f32[3,34,4,1]{1,3,2,0:T(1,128)S(1)}, u32[]{:S(2)}, u32[]{:S(2)}) collective-permute-start(f32[3,34,4,1]{1,3,2,0:T(1,128)S(1)} %get-tuple-element.22), channel_id=1, source_target_pairs={{0,1},{2,3},{4,5},{6,7},{8,9},{10,11},{12,13},{14,15},{16,17},{18,... | collective-permute-start | bytes 4904 | tf_op jit(solution)/shard_map/ppermute | solution.py:17
  97.2 6.4 %collective-permute-start.17 = (f32[3,34,4,1]{1,3,2,0:T(1,128)S(1)}, f32[3,34,4,1]{1,3,2,0:T(1,128)S(1)}, u32[]{:S(2)}, u32[]{:S(2)}) collective-permute-start(f32[3,34,4,1]{1,3,2,0:T(1,128)S(1)} %get-tuple-element.23), channel_id=1, source_target_pairs={{1,0},{3,2},{5,4},{7,6},{9,8},{11,10},{13,12},{15,14},{17,16},{19,... | collective-permute-start | bytes 4904 | tf_op jit(solution)/shard_map/ppermute | solution.py:19
  98.6 7.0 %collective-permute-start.8 = (bf16[258,1,128]{2,0,1:T(8,128)(2,1)S(1)}, bf16[258,1,128]{2,0,1:T(8,128)(2,1)S(1)}, u32[]{:S(2)}, u32[]{:S(2)}) collective-permute-start(bf16[258,1,128]{2,0,1:T(8,128)(2,1)S(1)} %get-tuple-element.18), channel_id=1, source_target_pairs={{0,2},{2,4},{4,6},{1,3},{3,5},{5,7},{8,10},{10,12},{12,14},{9,11},... | collective-permute-start | bytes 198152 | tf_op jit(solution)/shard_map/ppermute | solution.py:17
  102.1 6.8 %collective-permute-start.9 = (bf16[258,1,128]{2,0,1:T(8,128)(2,1)S(1)}, bf16[258,1,128]{2,0,1:T(8,128)(2,1)S(1)}, u32[]{:S(2)}, u32[]{:S(2)}) collective-permute-start(bf16[258,1,128]{2,0,1:T(8,128)(2,1)S(1)} %get-tuple-element.19), channel_id=1, source_target_pairs={{2,0},{4,2},{6,4},{3,1},{5,3},{7,5},{10,8},{12,10},{14,12},{11,9},... | collective-permute-start | bytes 198152 | tf_op jit(solution)/shard_map/ppermute | solution.py:19
  111.0 8.5 %copy-start.6 = (pred[128]{0:T(512)(128)(4,1)S(1)}, pred[128]{0:T(512)(128)(4,1)}, u32[]{:S(2)}) copy-start(pred[128]{0:T(512)(128)(4,1)} %get-tuple-element.53) | copy-start | bytes 388
  111.0 8.5 %copy-start.7 = (s32[128]{0:T(128)S(1)}, s32[128]{0:T(128)}, u32[]{:S(2)}) copy-start(s32[128]{0:T(128)} %get-tuple-element.50) | copy-start | bytes 1540
  111.0 8.5 %copy-start.8 = (s32[128]{0:T(128)S(1)}, s32[128]{0:T(128)}, u32[]{:S(2)}) copy-start(s32[128]{0:T(128)} %get-tuple-element.51) | copy-start | bytes 1540
  111.0 8.5 %copy-start.9 = (f32[128]{0:T(128)S(1)}, f32[128]{0:T(128)}, u32[]{:S(2)}) copy-start(f32[128]{0:T(128)} %get-tuple-element.48) | copy-start | bytes 1540
  111.1 8.5 %copy-start.10 = (f32[128]{0:T(128)S(1)}, f32[128]{0:T(128)}, u32[]{:S(2)}) copy-start(f32[128]{0:T(128)} %get-tuple-element.49) | copy-start | bytes 1540
  111.1 8.5 %copy-start.13 = (f32[128]{0:T(128)S(1)}, f32[128]{0:T(128)}, u32[]{:S(2)}) copy-start(f32[128]{0:T(128)} %fusion.119) | copy-start | bytes 1540
  115.2 16.9 %collective-permute-start.11 = (bf16[258,18,1]{0,1,2:T(8,128)(2,1)S(1)}, bf16[258,18,1]{0,1,2:T(8,128)(2,1)S(1)}, u32[]{:S(2)}, u32[]{:S(2)}) collective-permute-start(bf16[258,18,1]{0,1,2:T(8,128)(2,1)S(1)} %copy.121), channel_id=1, source_target_pairs={{1,0},{3,2},{5,4},{7,6},{9,8},{11,10},{13,12},{15,14},{17,16},{19,... | collective-permute-start | bytes 27872 | tf_op jit(solution)/shard_map/ppermute | solution.py:19
  116.5 15.1 %collective-permute-start.10 = (bf16[258,18,1]{0,1,2:T(8,128)(2,1)S(1)}, bf16[258,18,1]{0,1,2:T(8,128)(2,1)S(1)}, u32[]{:S(2)}, u32[]{:S(2)}) collective-permute-start(bf16[258,18,1]{0,1,2:T(8,128)(2,1)S(1)} %copy.120), channel_id=1, source_target_pairs={{0,1},{2,3},{4,5},{6,7},{8,9},{10,11},{12,13},{14,15},{16,17},{18,... | collective-permute-start | bytes 27872 | tf_op jit(solution)/shard_map/ppermute | solution.py:17
  133.7 4.6 %copy-start = (f32[3,256,16,128]{3,1,2,0:T(8,128)S(1)}, f32[3,256,16,128]{3,1,2,0:T(8,128)}, u32[]{:S(2)}) copy-start(f32[3,256,16,128]{3,1,2,0:T(8,128)} %fusion.10) | copy-start | bytes 18874372
  133.7 4.6 %copy-start.3 = (bf16[256,16,128]{2,1,0:T(8,128)(2,1)S(1)}, bf16[256,16,128]{2,1,0:T(8,128)(2,1)}, u32[]{:S(2)}) copy-start(bf16[256,16,128]{2,1,0:T(8,128)(2,1)} %param.4) | copy-start | bytes 3145732
where the time goes:
time: 145 us; the launch traced here: 144 us
  other arithmetic  44.2 us (30%)
  starting transfers between devices  41.2 us (28%)
  local copies, waits for them, and re-layouts  16 us (11%)
  waiting for transfers between devices  15.5 us (11%)
  matrix products  15.4 us (11%)
  blocking collectives  10.8 us (7%)
    ppermute x9, starting transfers between devices, padded_2(): lax.ppermute(tail, axis, [(i, (i + 1) % count) for i in range(ends)])  29.4 us
    ppermute x9, waiting for transfers between devices, padded_2(): lax.ppermute(head, axis, [((i + 1) % count, i) for i in range(ends)])  15.3 us
    another operation x3, other arithmetic, on_device(): factor = jnp.linalg.cholesky(line_matrix(lines))  12.4 us
    dot_general x1, matrix products, on_device(): jnp.einsum('nijc,kc->nijk', field, table_z, precision=lax.Precision.HIGHEST)  12 us
    another operation x2, other arithmetic, line_solve(): solved = jax.scipy.linalg.cho_solve((factor, True), flat)  11.9 us
    ppermute x9, starting transfers between devices, padded_2(): lax.ppermute(head, axis, [((i + 1) % count, i) for i in range(ends)])  11.8 us
    all_gather x1, blocking collectives, on_device(): whole = lax.all_gather(rhs, 'gx', axis=1, tiled=True)  10.8 us
    convert_element_type x1, other arithmetic, on_device(): grads = central(fine_padded.astype(jnp.float32))  4.58 us
  transfers between devices with their start and end apart: 18, of which 5 were waited for; matrix products, arithmetic and copies ran while one was open for 38% of the time, Pallas kernels for 0%

commit v1 on v0

v1 whole, which is shorter than its diff:
```python
import functools

import jax
import jax.numpy as jnp
import numpy as np
from jax import lax
from jax.experimental import pallas as pl
from jax.experimental.pallas import tpu as pltpu
from jax.sharding import PartitionSpec as P

stiffness = 64.0
BIN = 8
SLOT = 32
MESH = pl.DeviceIdType.MESH
HIGHEST = lax.Precision.HIGHEST


def inverse_table(devices, cells):
    lines = devices * cells
    theta = np.arccosh((1.0 + 2.0 * stiffness) / (2.0 * stiffness))
    index = np.arange(lines)
    low = np.minimum(index[:, None], index[None, :])
    high = np.maximum(index[:, None], index[None, :])
    a, b, c = (low + 1) * theta, (lines - high) * theta, (lines + 1) * theta
    inverse = (
        np.exp(a + b - c) * (1 - np.exp(-2 * a)) * (1 - np.exp(-2 * b)) / (1 - np.exp(-2 * c))
        / (2.0 * stiffness * np.sinh(theta))
    )
    table = np.zeros((devices, 3, cells + 16, cells + 8 * devices))
    sums = np.zeros((devices, 8, 3 * cells))
    for me in range(devices):
        first, last = me * cells, (me + 1) * cells - 1
        own = index[first : last + 1]
        up = np.exp((own - last) * theta) * (1 - np.exp(-2 * (own + 1) * theta)) / (1 - np.exp(-2 * (last + 1) * theta))
        down = (
            np.exp((first - own) * theta)
            * (1 - np.exp(-2 * (lines - own) * theta))
            / (1 - np.exp(-2 * (lines - first) * theta))
        )
        for k in range(3):
            sums[me, 2 * k, k * cells : (k + 1) * cells] = up
            sums[me, 2 * k + 1, k * cells : (k + 1) * cells] = down
            for row in range(7, cells + 9):
                x = first + row - 8
                if x < 0 or x >= lines:
                    continue
                table[me, k, row, :cells] = inverse[x, first : last + 1]
                for peer in range(devices):
                    if peer < me:
                        table[me, k, row, cells + 8 * peer + 2 * k] = inverse[x, (peer + 1) * cells - 1]
                    if peer > me:
                        table[me, k, row, cells + 8 * peer + 2 * k + 1] = inverse[x, peer * cells]
    return table.astype(np.float32), sums.astype(np.float32)


def lane_tables(cells_z, size_z, slots):
    place = np.zeros((cells_z, 3 * 128), np.float32)
    for variant in range(3):
        for z in range(cells_z):
            lane = z + 2 - (variant - 1) * cells_z
            if 0 <= lane < cells_z + 4:
                place[z, variant * 128 + lane] = 1.0
    binning = np.repeat(place, BIN, axis=0) / 32.0
    prolong = np.zeros((128, slots * size_z), np.float32)
    for slot in range(slots):
        for fine in range(size_z):
            lane, offset = slot * SLOT + fine // BIN + 2, (fine % BIN + 0.5) / BIN - 0.5
            prolong[lane, slot * size_z + fine] = 1.0 - abs(offset)
            prolong[lane + (1 if offset >= 0 else -1), slot * size_z + fine] = abs(offset)
    return place, binning, prolong


def kernel(
    counts,
    ref_ref, def_ref, disp_ref, table_ref, sums_ref, place_ref, bin_ref, prolong_ref,
    new_ref, out_ref,
    volume, binned, packed, halo, mine, theirs, xhalo, ysend, yhalo, zhalo, lines,
    near_send, near_recv, peer_send, peer_recv, x_send, x_recv, y_send, y_recv, z_send, z_recv,
):
    nx, ny, nz = counts
    sizex, sizey, sizez = ref_ref.shape
    cells_x, cells_z = sizex // BIN, sizez // BIN
    pitch = sizey + 16
    me = (lax.axis_index("gx"), lax.axis_index("gy"), lax.axis_index("gz"))

    def inside(offset):
        good = None
        for at, step, count in zip(me, offset, counts):
            if step:
                test = at > 0 if step < 0 else at < count - 1
                good = test if good is None else jnp.logical_and(good, test)
        return good

    def device(offset):
        return {"gx": me[0] + offset[0], "gy": me[1] + offset[1], "gz": me[2] + offset[2]}

    def peer(j):
        return {"gx": lax.rem(me[0] + j, nx), "gy": me[1], "gz": me[2]}

    steps = (-1, 0, 1)
    offsets = [(i, j, k) for i in steps for j in steps for k in steps if (i, j, k) != (0, 0, 0)]

    halo[...] = jnp.zeros_like(halo)
    theirs[...] = jnp.zeros_like(theirs)
    xhalo[...] = jnp.zeros_like(xhalo)
    yhalo[...] = jnp.zeros_like(yhalo)

    z_steps = (1,) if nz == 2 else (1, nz - 1)

    def z_device(step):
        return {"gx": me[0], "gy": me[1], "gz": lax.rem(me[2] + step, nz)}

    barrier = pltpu.get_barrier_semaphore()
    for j in range(1, nx):
        pl.semaphore_signal(barrier, inc=1, device_id=peer(j), device_id_type=MESH)
    expect = jnp.int32(nx - 1)
    for offset in offsets:
        if offset[1:] == (0, 0):
            continue

        @pl.when(inside(offset))
        def _():
            pl.semaphore_signal(barrier, inc=1, device_id=device(offset), device_id_type=MESH)

    reach = [
        1 + (at > 0).astype(jnp.int32) + (at < count - 1).astype(jnp.int32)
        for at, count in zip(me, counts)
    ]
    expect = expect + reach[0] * (reach[1] * reach[2] - 1)
    if nz > 2:
        ends = jnp.logical_or(me[2] == 0, me[2] == nz - 1)

        @pl.when(ends)
        def _():
            other = {"gx": me[0], "gy": me[1], "gz": nz - 1 - me[2]}
            pl.semaphore_signal(barrier, inc=1, device_id=other, device_id_type=MESH)

        expect = expect + ends.astype(jnp.int32)
    pl.semaphore_wait(barrier, expect)

    z_copies = [
        pltpu.make_async_remote_copy(
            src_ref=ref_ref, dst_ref=zhalo.at[i], send_sem=z_send.at[i], recv_sem=z_recv.at[i],
            device_id=z_device(step), device_id_type=MESH,
        )
        for i, step in enumerate(z_steps)
    ]

    source_rows = {-1: (0, 8), 0: (0, cells_x), 1: (cells_x - 8, 8)}
    target_rows = {-1: (0, 8), 0: (8, cells_x), 1: (cells_x + 8, 8)}

    def number(offset):
        return (offset[0] + 1) * 9 + (offset[1] + 1) * 3 + offset[2] + 1

    def near_copy(offset, part):
        blocks = pl.ds(0, 1) if part == 0 else pl.ds(1, 2)
        back = tuple(-step for step in offset)
        start, rows = source_rows[offset[0]]
        goal = target_rows[back[0]][0]
        return pltpu.make_async_remote_copy(
            src_ref=packed.at[offset[2] + 1, blocks, pl.ds(start, rows), :],
            dst_ref=halo.at[back[1] + 1, back[2] + 1, blocks, pl.ds(goal, rows), :],
            send_sem=near_send.at[number(offset), part],
            recv_sem=near_recv.at[number(back), part],
            device_id=device(offset), device_id_type=MESH,
        )

    def near_arrival(offset, part):
        blocks = pl.ds(0, 1) if part == 0 else pl.ds(1, 2)
        goal, rows = target_rows[offset[0]]
        where = halo.at[offset[1] + 1, offset[2] + 1, blocks, pl.ds(goal, rows), :]
        return pltpu.make_async_remote_copy(
            src_ref=where, dst_ref=where,
            send_sem=near_send.at[number(offset), part],
            recv_sem=near_recv.at[number(offset), part],
            device_id=device(offset), device_id_type=MESH,
        )

    def pack(lines_of):
        total = None
        for q, line in enumerate(lines_of):
            spread = jnp.dot(line, place_ref[...], precision=HIGHEST, preferred_element_type=jnp.float32)
            spread = [spread[:, 128 * v : 128 * (v + 1)] for v in range(3)]
            if q:
                spread = [pltpu.roll(s, SLOT * q, 1) for s in spread]
            total = spread if total is None else [t + s for t, s in zip(total, spread)]
        return total

    pairs = [(k, y) for k in range(3) for y in range(2)]
    for block, members in ((1, pairs[:4]), (2, pairs[4:])):
        spread = pack([disp_ref[k, :, y, :] for k, y in members])
        for v in range(3):
            packed[v, block] = spread[v]
        halo[1, 1, block, pl.ds(8, cells_x), :] = spread[1]
    for offset in offsets:

        @pl.when(inside(offset))
        def _():
            near_copy(offset, 1).start()

    def x_copy(step):
        return pltpu.make_async_remote_copy(
            src_ref=ref_ref.at[pl.ds(sizex - 1 if step > 0 else 0, 1)],
            dst_ref=xhalo.at[pl.ds(0 if step > 0 else 1, 1)],
            send_sem=x_send.at[0 if step > 0 else 1], recv_sem=x_recv.at[0 if step > 0 else 1],
            device_id=device((step, 0, 0)), device_id_type=MESH,
        )

    for step in (-1, 1):

        @pl.when(inside((step, 0, 0)))
        def _():
            x_copy(step).start()

    for copy in z_copies:
        copy.start()

    def bin_cell(cell, carry):
        rows = pl.multiple_of(cell * 8, 8)
        total = [None, None]
        for i in range(BIN):
            x = cell * BIN + i
            slabs = (ref_ref[x].astype(jnp.float32), def_ref[x].astype(jnp.float32))
            volume[pl.ds(pl.multiple_of((x + 1) * pitch + 8, 8), sizey), :] = slabs[0]
            total = [s if t is None else t + s for t, s in zip(total, slabs)]
        for image in range(2):
            for y in range(2):
                binned[2 * image + y, pl.ds(rows, 8), :] = total[image][8 * y : 8 * y + 8]
        return carry

    lax.fori_loop(0, cells_x, bin_cell, 0)
    spread = None
    for q in range(4):
        line = binned[q, pl.ds(0, cells_x, stride=8), :]
        for s in range(1, 8):
            line = line + binned[q, pl.ds(s, cells_x, stride=8), :]
        part = jnp.dot(line, bin_ref[...], precision=HIGHEST, preferred_element_type=jnp.float32)
        part = [part[:, 128 * v : 128 * (v + 1)] for v in range(3)]
        if q:
            part = [pltpu.roll(p, SLOT * q, 1) for p in part]
        spread = part if spread is None else [a + b for a, b in zip(spread, part)]
    for v in range(3):
        packed[v, 0] = spread[v]
    halo[1, 1, 0, pl.ds(8, cells_x), :] = spread[1]
    for offset in offsets:

        @pl.when(inside(offset))
        def _():
            near_copy(offset, 0).start()

    def y_copy(step):
        side = 1 if step > 0 else 0
        return pltpu.make_async_remote_copy(
            src_ref=ysend.at[side], dst_ref=yhalo.at[1 - side],
            send_sem=y_send.at[side], recv_sem=y_recv.at[1 - side],
            device_id=device((0, step, 0)), device_id_type=MESH,
        )

    ysend[0] = volume[pl.ds(pitch + 8, sizex, stride=pitch), :].astype(jnp.bfloat16)
    ysend[1] = volume[pl.ds(pitch + 7 + sizey, sizex, stride=pitch), :].astype(jnp.bfloat16)
    for step in (-1, 1):

        @pl.when(inside((0, step, 0)))
        def _():
            y_copy(step).start()

    for part in (1, 0):
        for offset in offsets:

            @pl.when(inside(offset))
            def _():
                near_arrival(offset, part).wait_recv()

    summed = [[halo[y, 0, b] + halo[y, 1, b] + halo[y, 2, b] for b in range(3)] for y in range(3)]
    rows = cells_x + 16
    lane = lax.broadcasted_iota(jnp.int32, (rows, 128), 1)
    slot = lane // SLOT

    def centred(b, upper):
        one, two = (SLOT, 128 - SLOT) if upper else (128 - SLOT, SLOT)
        ends = jnp.where(slot == 0, pltpu.roll(summed[0][b], one, 1), pltpu.roll(summed[2][b], one, 1))
        return jnp.where(jnp.logical_or(slot == 0, slot == 3), ends, pltpu.roll(summed[1][b], two, 1))

    coarse = centred(0, False)
    deformed = centred(0, True)
    displacement = [centred(1, False), centred(1, True), centred(2, False)]
    before = jnp.where(slot < 2, summed[0][0], pltpu.roll(summed[1][0], 64, 1))
    after = jnp.where(slot < 2, summed[1][0], pltpu.roll(summed[2][0], 64, 1))
    slopes = [
        (pltpu.roll(coarse, rows - 1, 0) - pltpu.roll(coarse, 1, 0)) * 0.5,
        (after - before) * 0.5,
        (pltpu.roll(coarse, 127, 1) - pltpu.roll(coarse, 1, 1)) * 0.5,
    ]
    mismatch = deformed - coarse - (
        slopes[0] * displacement[0] + slopes[1] * displacement[1] + slopes[2] * displacement[2]
    )
    place = lane - slot * SLOT
    low = jnp.where(me[2] > 0, 1, 2)
    high = jnp.where(me[2] < nz - 1, cells_z + 2, cells_z + 1)
    keep = jnp.logical_and(place >= low, place <= high)
    keep = jnp.logical_and(keep, slot >= jnp.where(me[1] > 0, 0, 1))
    keep = jnp.logical_and(keep, slot <= jnp.where(me[1] < ny - 1, 3, 2))
    rhs = [jnp.where(keep, s * mismatch, 0.0)[8 : 8 + cells_x] for s in slopes]

    mine[...] = jnp.dot(
        sums_ref[me[0]], jnp.concatenate(rhs, axis=0), precision=HIGHEST, preferred_element_type=jnp.float32
    )

    def peer_copy(j):
        return pltpu.make_async_remote_copy(
            src_ref=mine, dst_ref=theirs.at[me[0]],
            send_sem=peer_send.at[j], recv_sem=peer_recv.at[j],
            device_id=peer(j), device_id_type=MESH,
        )

    for j in range(1, nx):
        peer_copy(j).start()

    for step in (-1, 1):

        @pl.when(inside((step, 0, 0)))
        def _():
            x_copy(-step).wait_recv()

        @pl.when(inside((0, step, 0)))
        def _():
            y_copy(-step).wait_recv()

    volume[pl.ds(8, sizey), :] = xhalo[0].astype(jnp.float32)
    volume[pl.ds((sizex + 1) * pitch + 8, sizey), :] = xhalo[1].astype(jnp.float32)
    volume[pl.ds(pitch + 7, sizex, stride=pitch), :] = yhalo[0].astype(jnp.float32)
    volume[pl.ds(pitch + 8 + sizey, sizex, stride=pitch), :] = yhalo[1].astype(jnp.float32)

    row = lax.broadcasted_iota(jnp.int32, (sizez, sizez), 0)
    column = lax.broadcasted_iota(jnp.int32, (sizez, sizez), 1)
    inner = jnp.where(row == column + 1, 1.0, 0.0) - jnp.where(row + 1 == column, 1.0, 0.0)
    from_low = jnp.where(
        jnp.logical_and(jnp.logical_and(row == sizez - 1, column == 0), me[2] > 0), -1.0, 0.0
    )
    from_high = jnp.where(
        jnp.logical_and(jnp.logical_and(row == 0, column == sizez - 1), me[2] < nz - 1), 1.0, 0.0
    )
    outer = [from_low + from_high] if nz == 2 else [from_low, from_high]
    across = jnp.concatenate([inner] + outer, axis=0).astype(jnp.bfloat16)

    for j in range(1, nx):
        came = pltpu.make_async_remote_copy(
            src_ref=mine, dst_ref=theirs.at[lax.rem(me[0] + nx - j, nx)],
            send_sem=peer_send.at[j], recv_sem=peer_recv.at[j],
            device_id=peer(j), device_id_type=MESH,
        )
        came.wait_recv()

    sums = theirs[...].reshape(8 * nx, 128)
    for k in range(3):
        step = jnp.dot(
            table_ref[me[0], k], jnp.concatenate([rhs[k], sums], axis=0),
            precision=HIGHEST, preferred_element_type=jnp.float32,
        )
        new = displacement[k] + step
        for y in range(2):
            shift = 128 - SLOT * (y + 1) - 2
            new_ref[k, :, y, :] = pltpu.roll(new, shift, 1)[8 : 8 + cells_x, :cells_z]
        along = jnp.dot(new, prolong_ref[...], precision=HIGHEST, preferred_element_type=jnp.float32) * 0.5
        for s in range(4):
            lines[k, s] = along[:, sizez * s : sizez * (s + 1)]

    for copy in z_copies:
        copy.wait_recv()

    third = lax.broadcasted_iota(jnp.int32, (8, sizez), 0).astype(jnp.float32)
    offset_y = (third + 0.5) / 8.0 - 0.5
    weight_low = jnp.maximum(-offset_y, 0.0)
    weight_high = jnp.maximum(offset_y, 0.0)
    weight_mid = 1.0 - jnp.abs(offset_y)

    def plane(at):
        planes = []
        for k in range(3):
            row_of = [lines[k, s, pl.ds(at, 1), :] for s in range(4)]
            planes.append(
                jnp.concatenate(
                    [
                        weight_low * row_of[c] + weight_mid * row_of[c + 1] + weight_high * row_of[c + 2]
                        for c in range(2)
                    ],
                    axis=0,
                )
            )
        return planes

    def residual(cell, carry):
        past, now = carry
        later = plane(cell + 9)
        slabs = pl.ds(cell * BIN, BIN)
        images = [ref_ref[slabs].reshape(BIN * sizey, sizez)] + [
            zhalo[i, slabs].reshape(BIN * sizey, sizez) for i in range(len(z_steps))
        ]
        grad_z = jnp.dot(jnp.concatenate(images, axis=1), across, preferred_element_type=jnp.float32)
        for i in range(BIN):
            t = (i + 0.5) / BIN - 0.5
            other = later if t > 0 else past
            field = [n + abs(t) * (o - n) for n, o in zip(now, other)]
            x = cell * BIN + i
            base = pl.multiple_of((x + 1) * pitch, 8)
            centre = volume[pl.ds(base + 8, sizey), :]
            grad_x = volume[pl.ds(base + pitch + 8, sizey), :] - volume[pl.ds(base - pitch + 8, sizey), :]
            grad_y = volume[pl.ds(base + 9, sizey), :] - volume[pl.ds(base + 7, sizey), :]
            total = def_ref[x].astype(jnp.float32) - centre
            total = total - grad_x * field[0] - grad_y * field[1]
            total = total - grad_z[i * sizey : (i + 1) * sizey] * field[2]
            out_ref[x] = total.astype(jnp.bfloat16)
        return (now, later)

    lax.fori_loop(0, cells_x, residual, (plane(7), plane(8)))

    for copy in z_copies:
        copy.wait_send()
    for j in range(1, nx):
        peer_copy(j).wait_send()
    for step in (-1, 1):

        @pl.when(inside((step, 0, 0)))
        def _():
            x_copy(step).wait_send()

        @pl.when(inside((0, step, 0)))
        def _():
            y_copy(step).wait_send()

    for offset in offsets:

        @pl.when(inside(offset))
        def _():
            for part in range(2):
                near_copy(offset, part).wait_send()


def on_device(counts, ref_image, def_image, displacement):
    nx, ny, nz = counts
    sizex, sizey, sizez = ref_image.shape
    cells_x, cells_z = sizex // BIN, sizez // BIN
    table, sums = inverse_table(nx, cells_x)
    place, binning, prolong = lane_tables(cells_z, sizez, 4)
    sides = 1 if nz == 2 else 2
    dma = pltpu.SemaphoreType.DMA
    vmem = pl.BlockSpec(memory_space=pltpu.VMEM)
    return pl.pallas_call(
        functools.partial(kernel, counts),
        out_shape=(
            jax.ShapeDtypeStruct(displacement.shape, jnp.float32),
            jax.ShapeDtypeStruct(ref_image.shape, jnp.bfloat16),
        ),
        in_specs=[vmem] * 8,
        out_specs=(vmem, vmem),
        scratch_shapes=[
            pltpu.VMEM(((sizex + 2) * (sizey + 16), sizez), jnp.float32),
            pltpu.VMEM((4, cells_x * 8, sizez), jnp.float32),
            pltpu.VMEM((3, 3, cells_x, 128), jnp.float32),
            pltpu.VMEM((3, 3, 3, cells_x + 16, 128), jnp.float32),
            pltpu.VMEM((8, 128), jnp.float32),
            pltpu.VMEM((nx, 8, 128), jnp.float32),
            pltpu.VMEM((2, sizey, sizez), jnp.bfloat16),
            pltpu.VMEM((2, sizex, sizez), jnp.bfloat16),
            pltpu.VMEM((2, sizex, sizez), jnp.bfloat16),
            pltpu.VMEM((sides, sizex, sizey, sizez), jnp.bfloat16),
            pltpu.VMEM((3, 4, cells_x + 16, sizez), jnp.float32),
            dma((27, 2)), dma((27, 2)), dma((nx,)), dma((nx,)),
            dma((2,)), dma((2,)), dma((2,)), dma((2,)), dma((sides,)), dma((sides,)),
        ],
        compiler_params=pltpu.CompilerParams(collective_id=0, has_side_effects=True),
    )(ref_image, def_image, displacement, table, sums, place, binning, prolong)


def solution(mesh):
    counts = tuple(mesh.shape[axis] for axis in ("gx", "gy", "gz"))
    return jax.shard_map(
        functools.partial(on_device, counts),
        mesh=mesh,
        in_specs=(P("gx", "gy", "gz"), P("gx", "gy", "gz"), P(None, "gx", "gy", "gz")),
        out_specs=(P(None, "gx", "gy", "gz"), P("gx", "gy", "gz")),
        check_vma=False,
    )
```

time: 145 us -> 32 us (0.22)
  other arithmetic: 44.2 us -> 0 us
  starting transfers between devices: 41.2 us -> 0 us
  Pallas kernels: 0 us -> 25.6 us
  waiting for transfers between devices: 15.5 us -> 0 us
  matrix products: 15.4 us -> 0 us
  blocking collectives: 10.8 us -> 0 us
  local copies, waits for them, and re-layouts: 16 us -> 5.5 us
    ppermute x18 -> x0, starting transfers between devices: 41.2 us -> none  [the longest x9 29.4 us: padded_2(): lax.ppermute(tail, axis, [(i, (i + 1) % count) for i in range(ends)])]
    pallas_call x0 -> x1, Pallas kernels: none -> 25.6 us  [on_device(): pl.pallas_call(functools.partial(kernel, counts), out_shape=(jax.ShapeDty...]
    another operation x6 -> x0, other arithmetic: 24.3 us -> none  [the longest x3 12.4 us: on_device(): factor = jnp.linalg.cholesky(line_matrix(lines))]
    ppermute x18 -> x0, waiting for transfers between devices: 15.5 us -> none  [the longest x9 15.3 us: padded_2(): lax.ppermute(head, axis, [((i + 1) % count, i) for i in range(ends)])]
    dot_general x5 -> x0, matrix products: 14.8 us -> none  [the longest x1 12 us: on_device(): jnp.einsum('nijc,kc->nijk', field, table_z, precision=lax.Precision.HIGHEST)]
    all_gather x1 -> x0, blocking collectives: 10.8 us -> none  [on_device(): whole = lax.all_gather(rhs, 'gx', axis=1, tiled=True)]
    convert_element_type x2 -> x0, other arithmetic: 8.9 us -> none  [the longest x1 4.58 us: on_device(): grads = central(fine_padded.astype(jnp.float32))]
    slice x8 -> x0, local copies, waits for them, and re-layouts: 6.17 us -> none  [the longest x6 4.03 us: padded_2(): lax.slice_in_dim(cells, cells.shape[dim] - width, cells.shape[dim], axis=...]
  transfers between devices with their start and end apart: 18 -> 0, of which waited for: 5 -> 0; matrix products, arithmetic and copies ran while one was open for 38% -> 0% of each run, Pallas kernels for 0% -> 0%
where the time goes in v1:
time: 32 us; the launch traced here: 31.7 us
  Pallas kernels  25.6 us (80%)
  local copies, waits for them, and re-layouts  5.5 us (17%)
  between operations  0.64 us (2%)
    pallas_call x1, Pallas kernels, on_device(): pl.pallas_call(functools.partial(kernel, counts), out_shape=(jax.ShapeDty...  25.6 us
    unnamed x2, local copies, waits for them, and re-layouts  3.9 us
    pallas_call x1, local copies, waits for them, and re-layouts, on_device(): pl.pallas_call(functools.partial(kernel, counts), out_shape=(jax.ShapeDty...  1.6 us

profile of v1, /device:TPU:0, one launch (start us, length us, event | category | flops | bytes accessed | tf_op | source)
XLA Modules:
  0.0 31.7 jit_solution(4315229240235057912)
XLA Ops:
  0.6 1.5 %copy.10.disp_ref = f32[3,32,2,16]{3,2,1,0:T(2,128)} copy(f32[3,32,2,16]{1,3,2,0:T(8,128)} %param.10) | data formatting | bytes 24576 | tf_op args[2]
  2.2 25.6 %shard_map.95 = (f32[3,32,2,16]{3,2,1,0:T(2,128)}, bf16[256,16,128]{2,1,0:T(8,128)(2,1)}) custom-call(bf16[256,16,128]{2,1,0:T(8,128)(2,1)} %ref_ref.1, bf16[256,16,128]{2,1,0:T(8,128)(2,1)} %def_ref.1, f32[3,32,2,16]{3,2,1,0:T(2,128)} %copy.10.disp_ref, f32[4,3,48,64]{3,2,1,0:T(8,128)} %constant.10.clone.table_ref, f32[4,8,96]{2,1,0:T(8,128)} %constant.11.clone.sums_ref, ...), custom_call_target="tpu_custom_call" | custom-call | tf_op jit(solution)/shard_map/pallas_call | solution.py:448
  27.7 1.6 %copy.11 = f32[3,32,2,16]{1,3,2,0:T(8,128)} copy(f32[3,32,2,16]{3,2,1,0:T(2,128)} %get-tuple-element.2) | data formatting | bytes 24576 | tf_op jit(solution)/shard_map/pallas_call | solution.py:448
  29.3 2.4 %copy.13 = bf16[256,16,128]{2,1,0:T(8,128)(2,1)} copy(bf16[256,16,128]{2,1,0:T(8,128)(2,1)} %get-tuple-element.7) | data formatting | bytes 2097152

commit v2 on v1

--- a/solution.py
+++ b/solution.py
@@ -70,17 +70,19 @@
     return place, binning, prolong
 
 
-def kernel(
+def exchange(
     counts,
-    ref_ref, def_ref, disp_ref, table_ref, sums_ref, place_ref, bin_ref, prolong_ref,
-    new_ref, out_ref,
-    volume, binned, packed, halo, mine, theirs, xhalo, ysend, yhalo, zhalo, lines,
+    ref_hbm, def_hbm, disp_hbm, table_hbm, sums_hbm, place_hbm, bin_hbm, prolong_hbm,
+    new_ref, lines, framed, def_ref, yout, zhalo,
+    disp_ref, table_ref, sums_ref, place_ref, bin_ref, prolong_ref,
+    binned, packed, halo, mine, theirs, xhalo, yrows, ysend, yhalo,
+    load_sem,
     near_send, near_recv, peer_send, peer_recv, x_send, x_recv, y_send, y_recv, z_send, z_recv,
 ):
     nx, ny, nz = counts
-    sizex, sizey, sizez = ref_ref.shape
+    sizex, sizey, sizez = def_ref.shape
+    ref_ref = framed.at[pl.ds(1, sizex)]
     cells_x, cells_z = sizex // BIN, sizez // BIN
-    pitch = sizey + 16
     me = (lax.axis_index("gx"), lax.axis_index("gy"), lax.axis_index("gz"))
 
     def inside(offset):
@@ -100,6 +102,18 @@
     steps = (-1, 0, 1)
     offsets = [(i, j, k) for i in steps for j in steps for k in steps if (i, j, k) != (0, 0, 0)]
 
+    loads = [
+        pltpu.make_async_copy(hbm, held, load_sem.at[i])
+        for i, (hbm, held) in enumerate(
+            (
+                (disp_hbm, disp_ref), (place_hbm, place_ref), (ref_hbm, ref_ref), (def_hbm, def_ref),
+                (bin_hbm, bin_ref), (sums_hbm.at[me[0]], sums_ref),
+                (table_hbm.at[me[0]], table_ref), (prolong_hbm, prolong_ref),
+            )
+        )
+    ]
+    for load in loads:
+        load.start()
     halo[...] = jnp.zeros_like(halo)
     theirs[...] = jnp.zeros_like(theirs)
     xhalo[...] = jnp.zeros_like(xhalo)
@@ -176,10 +190,16 @@
             device_id=device(offset), device_id_type=MESH,
         )
 
+    for load in loads[:2]:
+        load.wait()
+
     def pack(lines_of):
         total = None
         for q, line in enumerate(lines_of):
-            spread = jnp.dot(line, place_ref[...], precision=HIGHEST, preferred_element_type=jnp.float32)
+            spread = lax.dot_general(
+                line, place_ref[...], (((0,), (0,)), ((), ())),
+                precision=HIGHEST, preferred_element_type=jnp.float32,
+            )
             spread = [spread[:, 128 * v : 128 * (v + 1)] for v in range(3)]
             if q:
                 spread = [pltpu.roll(s, SLOT * q, 1) for s in spread]
@@ -188,7 +208,7 @@
 
     pairs = [(k, y) for k in range(3) for y in range(2)]
     for block, members in ((1, pairs[:4]), (2, pairs[4:])):
-        spread = pack([disp_ref[k, :, y, :] for k, y in members])
+        spread = pack([disp_ref[k, y] for k, y in members])
         for v in range(3):
             packed[v, block] = spread[v]
         halo[1, 1, block, pl.ds(8, cells_x), :] = spread[1]
@@ -206,6 +226,8 @@
             device_id=device((step, 0, 0)), device_id_type=MESH,
         )
 
+    for load in loads[2:4]:
+        load.wait()
     for step in (-1, 1):
 
         @pl.when(inside((step, 0, 0)))
@@ -221,7 +243,8 @@
         for i in range(BIN):
             x = cell * BIN + i
             slabs = (ref_ref[x].astype(jnp.float32), def_ref[x].astype(jnp.float32))
-            volume[pl.ds(pl.multiple_of((x + 1) * pitch + 8, 8), sizey), :] = slabs[0]
+            yrows[0, pl.ds(x, 1), :] = slabs[0][:1]
+            yrows[1, pl.ds(x, 1), :] = slabs[0][sizey - 1 :]
             total = [s if t is None else t + s for t, s in zip(total, slabs)]
         for image in range(2):
             for y in range(2):
@@ -229,6 +252,8 @@
         return carry
 
     lax.fori_loop(0, cells_x, bin_cell, 0)
+    for load in loads[4:]:
+        load.wait()
     spread = None
     for q in range(4):
         line = binned[q, pl.ds(0, cells_x, stride=8), :]
@@ -256,8 +281,7 @@
             device_id=device((0, step, 0)), device_id_type=MESH,
         )
 
-    ysend[0] = volume[pl.ds(pitch + 8, sizex, stride=pitch), :].astype(jnp.bfloat16)
-    ysend[1] = volume[pl.ds(pitch + 7 + sizey, sizex, stride=pitch), :].astype(jnp.bfloat16)
+    ysend[...] = yrows[...].astype(jnp.bfloat16)
     for step in (-1, 1):
 
         @pl.when(inside((0, step, 0)))
@@ -303,7 +327,7 @@
     rhs = [jnp.where(keep, s * mismatch, 0.0)[8 : 8 + cells_x] for s in slopes]
 
     mine[...] = jnp.dot(
-        sums_ref[me[0]], jnp.concatenate(rhs, axis=0), precision=HIGHEST, preferred_element_type=jnp.float32
+        sums_ref[...], jnp.concatenate(rhs, axis=0), precision=HIGHEST, preferred_element_type=jnp.float32
     )
 
     def peer_copy(j):
@@ -326,22 +350,9 @@
         def _():
             y_copy(-step).wait_recv()
 
-    volume[pl.ds(8, sizey), :] = xhalo[0].astype(jnp.float32)
-    volume[pl.ds((sizex + 1) * pitch + 8, sizey), :] = xhalo[1].astype(jnp.float32)
-    volume[pl.ds(pitch + 7, sizex, stride=pitch), :] = yhalo[0].astype(jnp.float32)
-    volume[pl.ds(pitch + 8 + sizey, sizex, stride=pitch), :] = yhalo[1].astype(jnp.float32)
-
-    row = lax.broadcasted_iota(jnp.int32, (sizez, sizez), 0)
-    column = lax.broadcasted_iota(jnp.int32, (sizez, sizez), 1)
-    inner = jnp.where(row == column + 1, 1.0, 0.0) - jnp.where(row + 1 == column, 1.0, 0.0)
-    from_low = jnp.where(
-        jnp.logical_and(jnp.logical_and(row == sizez - 1, column == 0), me[2] > 0), -1.0, 0.0
-    )
-    from_high = jnp.where(
-        jnp.logical_and(jnp.logical_and(row == 0, column == sizez - 1), me[2] < nz - 1), 1.0, 0.0
-    )
-    outer = [from_low + from_high] if nz == 2 else [from_low, from_high]
-    across = jnp.concatenate([inner] + outer, axis=0).astype(jnp.bfloat16)
+    framed[0] = xhalo[0]
+    framed[sizex + 1] = xhalo[1]
+    yout[...] = yhalo[...]
 
     for j in range(1, nx):
         came = pltpu.make_async_remote_copy(
@@ -351,22 +362,82 @@
         )
         came.wait_recv()
 
+    lane_of = lax.broadcasted_iota(jnp.int32, (cells_z, 128), 1)
+    z_of = lax.broadcasted_iota(jnp.int32, (cells_z, 128), 0)
     sums = theirs[...].reshape(8 * nx, 128)
     for k in range(3):
         step = jnp.dot(
-            table_ref[me[0], k], jnp.concatenate([rhs[k], sums], axis=0),
+            table_ref[k], jnp.concatenate([rhs[k], sums], axis=0),
             precision=HIGHEST, preferred_element_type=jnp.float32,
         )
         new = displacement[k] + step
         for y in range(2):
-            shift = 128 - SLOT * (y + 1) - 2
-            new_ref[k, :, y, :] = pltpu.roll(new, shift, 1)[8 : 8 + cells_x, :cells_z]
+            new_ref[k, y] = lax.dot_general(
+                jnp.where(lane_of == z_of + (SLOT * (y + 1) + 2), 1.0, 0.0), new[8 : 8 + cells_x],
+                (((1,), (1,)), ((), ())), precision=HIGHEST, preferred_element_type=jnp.float32,
+            )
         along = jnp.dot(new, prolong_ref[...], precision=HIGHEST, preferred_element_type=jnp.float32) * 0.5
         for s in range(4):
             lines[k, s] = along[:, sizez * s : sizez * (s + 1)]
 
     for copy in z_copies:
         copy.wait_recv()
+
+    for copy in z_copies:
+        copy.wait_send()
+    for j in range(1, nx):
+        peer_copy(j).wait_send()
+    for step in (-1, 1):
+
+        @pl.when(inside((step, 0, 0)))
+        def _():
+            x_copy(step).wait_send()
+
+        @pl.when(inside((0, step, 0)))
+        def _():
+            y_copy(step).wait_send()
+
+    for offset in offsets:
+
+        @pl.when(inside(offset))
+        def _():
+            for part in range(2):
+                near_copy(offset, part).wait_send()
+
+
+def combine(
+    counts, chunks,
+    new_in, lines, refs, defs, yhalo, zhalo,
+    new_ref, out_hbm,
+    out, out_sem,
+):
+    nz = counts[2]
+    sizex, sizey, sizez = defs.shape
+    cells_x = sizex // BIN
+    sides = zhalo.shape[0]
+    span = sizex // chunks
+    at_z = lax.axis_index("gz")
+    new_ref[...] = new_in[...]
+
+    row = lax.broadcasted_iota(jnp.int32, (sizez, sizez), 0)
+    column = lax.broadcasted_iota(jnp.int32, (sizez, sizez), 1)
+    inner = jnp.where(row == column + 1, 1.0, 0.0) - jnp.where(row + 1 == column, 1.0, 0.0)
+    from_low = jnp.where(
+        jnp.logical_and(jnp.logical_and(row == sizez - 1, column == 0), at_z > 0), -1.0, 0.0
+    )
+    from_high = jnp.where(
+        jnp.logical_and(jnp.logical_and(row == 0, column == sizez - 1), at_z < nz - 1), 1.0, 0.0
+    )
+    outer = [from_low + from_high] if sides == 1 else [from_low, from_high]
+    across = jnp.concatenate([inner] + outer, axis=0).astype(jnp.bfloat16)
+
+    rows = BIN * sizey
+    row = lax.broadcasted_iota(jnp.int32, (rows, rows + 16), 0)
+    column = lax.broadcasted_iota(jnp.int32, (rows, rows + 16), 1)
+    y, slab = row % sizey, row // sizey
+    after = jnp.where(y == sizey - 1, rows + 8 + slab, row + 1)
+    before = jnp.where(y == 0, rows + slab, row - 1)
+    along = (jnp.where(column == after, 1.0, 0.0) - jnp.where(column == before, 1.0, 0.0)).astype(jnp.bfloat16)
 
     third = lax.broadcasted_iota(jnp.int32, (8, sizez), 0).astype(jnp.float32)
     offset_y = (third + 0.5) / 8.0 - 0.5
@@ -392,48 +463,37 @@
     def residual(cell, carry):
         past, now = carry
         later = plane(cell + 9)
-        slabs = pl.ds(cell * BIN, BIN)
-        images = [ref_ref[slabs].reshape(BIN * sizey, sizez)] + [
-            zhalo[i, slabs].reshape(BIN * sizey, sizez) for i in range(len(z_steps))
-        ]
-        grad_z = jnp.dot(jnp.concatenate(images, axis=1), across, preferred_element_type=jnp.float32)
+        start = pl.multiple_of(cell * BIN, BIN)
+        own = refs[pl.ds(start + 1, BIN)].reshape(rows, sizez)
+        sideways = [own] + [zhalo[i, pl.ds(start, BIN)].reshape(rows, sizez) for i in range(sides)]
+        grad_z = jnp.dot(jnp.concatenate(sideways, axis=1), across, preferred_element_type=jnp.float32)
+        ends = jnp.concatenate([yhalo[i, pl.ds(start, BIN), :].astype(jnp.float32) for i in range(2)], axis=0)
+        grad_y = jnp.dot(
+            along, jnp.concatenate([own, ends.astype(jnp.bfloat16)], axis=0), preferred_element_type=jnp.float32
+        )
+        slabs = [refs[start + i].astype(jnp.float32) for i in range(BIN + 2)]
         for i in range(BIN):
             t = (i + 0.5) / BIN - 0.5
             other = later if t > 0 else past
             field = [n + abs(t) * (o - n) for n, o in zip(now, other)]
-            x = cell * BIN + i
-            base = pl.multiple_of((x + 1) * pitch, 8)
-            centre = volume[pl.ds(base + 8, sizey), :]
-            grad_x = volume[pl.ds(base + pitch + 8, sizey), :] - volume[pl.ds(base - pitch + 8, sizey), :]
-            grad_y = volume[pl.ds(base + 9, sizey), :] - volume[pl.ds(base + 7, sizey), :]
-            total = def_ref[x].astype(jnp.float32) - centre
-            total = total - grad_x * field[0] - grad_y * field[1]
-            total = total - grad_z[i * sizey : (i + 1) * sizey] * field[2]
-            out_ref[x] = total.astype(jnp.bfloat16)
+            part = slice(i * sizey, (i + 1) * sizey)
+            total = defs[start + i].astype(jnp.float32) - slabs[i + 1]
+            total = total - (slabs[i + 2] - slabs[i]) * field[0]
+            total = total - grad_y[part] * field[1] - grad_z[part] * field[2]
+            out[start + i] = total.astype(jnp.bfloat16)
         return (now, later)
 
-    lax.fori_loop(0, cells_x, residual, (plane(7), plane(8)))
-
-    for copy in z_copies:
-        copy.wait_send()
-    for j in range(1, nx):
-        peer_copy(j).wait_send()
-    for step in (-1, 1):
-
-        @pl.when(inside((step, 0, 0)))
-        def _():
-            x_copy(step).wait_send()
-
-        @pl.when(inside((0, step, 0)))
-        def _():
-            y_copy(step).wait_send()
-
-    for offset in offsets:
-
-        @pl.when(inside(offset))
-        def _():
-            for part in range(2):
-                near_copy(offset, part).wait_send()
+    def store(c):
+        slabs = pl.ds(c * span, span)
+        return pltpu.make_async_copy(out.at[slabs], out_hbm.at[slabs], out_sem.at[c])
+
+    state = (plane(7), plane(8))
+    for c in range(chunks):
+        each = cells_x // chunks
+        state = lax.fori_loop(c * each, (c + 1) * each, residual, state)
+        store(c).start()
+    for c in range(chunks):
+        store(c).wait()
 
 
 def on_device(counts, ref_image, def_image, displacement):
@@ -444,32 +504,57 @@
     place, binning, prolong = lane_tables(cells_z, sizez, 4)
     sides = 1 if nz == 2 else 2
     dma = pltpu.SemaphoreType.DMA
-    vmem = pl.BlockSpec(memory_space=pltpu.VMEM)
-    return pl.pallas_call(
-        functools.partial(kernel, counts),
+    vmem, anywhere = pl.BlockSpec(memory_space=pltpu.VMEM), pl.BlockSpec(memory_space=pl.ANY)
+    shape = jax.ShapeDtypeStruct
+    image = ref_image.shape
+    cells = jnp.transpose(displacement, (0, 2, 3, 1))
+    constants = (table, sums, place, binning, prolong)
+    held = pl.pallas_call(
+        functools.partial(exchange, counts),
         out_shape=(
-            jax.ShapeDtypeStruct(displacement.shape, jnp.float32),
-            jax.ShapeDtypeStruct(ref_image.shape, jnp.bfloat16),
+            shape(cells.shape, jnp.float32),
+            shape((3, 4, cells_x + 16, sizez), jnp.float32),
+            shape((sizex + 2, sizey, sizez), jnp.bfloat16),
+            shape(image, jnp.bfloat16),
+            shape((2, sizex, sizez), jnp.bfloat16),
+            shape((sides,) + image, jnp.bfloat16),
         ),
-        in_specs=[vmem] * 8,
-        out_specs=(vmem, vmem),
+        in_specs=[pl.BlockSpec(memory_space=pltpu.HBM)] * 8,
+        out_specs=(vmem,) * 5 + (anywhere,),
         scratch_shapes=[
-            pltpu.VMEM(((sizex + 2) * (sizey + 16), sizez), jnp.float32),
+            pltpu.VMEM(cells.shape, jnp.float32),
+            pltpu.VMEM(table.shape[1:], jnp.float32),
+            pltpu.VMEM(sums.shape[1:], jnp.float32),
+            pltpu.VMEM(place.shape, jnp.float32),
+            pltpu.VMEM(binning.shape, jnp.float32),
+            pltpu.VMEM(prolong.shape, jnp.float32),
             pltpu.VMEM((4, cells_x * 8, sizez), jnp.float32),
             pltpu.VMEM((3, 3, cells_x, 128), jnp.float32),
             pltpu.VMEM((3, 3, 3, cells_x + 16, 128), jnp.float32),
             pltpu.VMEM((8, 128), jnp.float32),
             pltpu.VMEM((nx, 8, 128), jnp.float32),
             pltpu.VMEM((2, sizey, sizez), jnp.bfloat16),
+            pltpu.VMEM((2, sizex, sizez), jnp.float32),
             pltpu.VMEM((2, sizex, sizez), jnp.bfloat16),
             pltpu.VMEM((2, sizex, sizez), jnp.bfloat16),
-            pltpu.VMEM((sides, sizex, sizey, sizez), jnp.bfloat16),
-            pltpu.VMEM((3, 4, cells_x + 16, sizez), jnp.float32),
+            dma((8,)),
             dma((27, 2)), dma((27, 2)), dma((nx,)), dma((nx,)),
             dma((2,)), dma((2,)), dma((2,)), dma((2,)), dma((sides,)), dma((sides,)),
         ],
-        compiler_params=pltpu.CompilerParams(collective_id=0, has_side_effects=True),
-    )(ref_image, def_image, displacement, table, sums, place, binning, prolong)
+        compiler_params=pltpu.CompilerParams(
+            collective_id=0, has_side_effects=True, vmem_limit_bytes=16 << 20
+        ),
+    )(*[pltpu.with_memory_space_constraint(jnp.asarray(x), pltpu.HBM) for x in (ref_image, def_image, cells) + constants])
+    chunks = 4
+    new, residual = pl.pallas_call(
+        functools.partial(combine, counts, chunks),
+        out_shape=(shape(cells.shape, jnp.float32), shape(image, jnp.bfloat16)),
+        in_specs=[vmem] * 6,
+        out_specs=(vmem, anywhere),
+        scratch_shapes=[pltpu.VMEM(image, jnp.bfloat16), dma((chunks,))],
+        compiler_params=pltpu.CompilerParams(vmem_limit_bytes=16 << 20),
+    )(*held)
+    return jnp.transpose(new, (0, 3, 1, 2)), residual
 
 
 def solution(mesh):

time: 32 us -> 25.8 us (0.81)
  local copies, waits for them, and re-layouts: 5.5 us -> 0 us
  Pallas kernels: 25.6 us -> 25 us
    unnamed x2 -> x0, local copies, waits for them, and re-layouts: 3.9 us -> none
    pallas_call x1 -> x0, local copies, waits for them, and re-layouts: 1.6 us -> none  [on_device(): pl.pallas_call(functools.partial(kernel, counts), out_shape=(jax.ShapeDty...]
    pallas_call x1 -> x2, Pallas kernels: 25.6 us -> 25 us  [the longest x1 17.7 us: on_device(): pl.pallas_call(functools.partial(exchange, counts), out_shape=(shape(cell...]
where the time goes in v2:
time: 25.8 us; the launch traced here: 25.6 us
  Pallas kernels  25 us (97%)
  between operations  0.64 us (2%)
    pallas_call x1, Pallas kernels, on_device(): pl.pallas_call(functools.partial(exchange, counts), out_shape=(shape(cell...  17.7 us
    pallas_call x1, Pallas kernels, on_device(): pl.pallas_call(functools.partial(combine, counts, chunks), out_shape=(sha...  7.25 us

profile of v2, /device:TPU:0, one launch (start us, length us, event | category | flops | bytes accessed | tf_op | source)
XLA Modules:
  0.0 25.6 jit_solution(14068975381183439714)
XLA Ops:
  0.6 17.7 %shard_map.95 = (f32[3,2,16,32]{3,2,1,0:T(8,128)S(1)}, f32[3,4,48,128]{3,2,1,0:T(8,128)S(1)}, bf16[258,16,128]{2,1,0:T(8,128)(2,1)S(1)}, bf16[256,16,128]{2,1,0:...) custom-call(bf16[256,16,128]{2,1,0:T(8,128)(2,1)} %ref_hbm.1, ...), custom_call_target="tpu_custom_call" | custom-call | tf_op jit(solution)/shard_map/pallas_call | solution.py:512
  18.4 7.2 %shard_map.96 = (f32[3,2,16,32]{3,2,1,0:T(8,128)}, bf16[256,16,128]{2,1,0:T(8,128)(2,1)}) custom-call(f32[3,2,16,32]{3,2,1,0:T(8,128)S(1)} %get-tuple-element.10.new_in, f32[3,4,48,128]{3,2,1,0:T(8,128)S(1)} %get-tuple-element.11.lines, bf16[258,16,128]{2,1,0:T(8,128)(2,1)S(1)} %get-tuple-element.12.refs, bf16[256,16,128]{2,1,0:T(8,128)(2,1)S(1)} %get-tuple-element.13.defs, ...), custom_call_target="tpu_custom_call" | custom-call | tf_op jit(solution)/shard_map/pallas_call | solution.py:549

commit v3 on v2

--- a/solution.py
+++ b/solution.py
@@ -150,8 +150,6 @@
             pl.semaphore_signal(barrier, inc=1, device_id=other, device_id_type=MESH)
 
         expect = expect + ends.astype(jnp.int32)
-    pl.semaphore_wait(barrier, expect)
-
     z_copies = [
         pltpu.make_async_remote_copy(
             src_ref=ref_ref, dst_ref=zhalo.at[i], send_sem=z_send.at[i], recv_sem=z_recv.at[i],
@@ -166,8 +164,11 @@
     def number(offset):
         return (offset[0] + 1) * 9 + (offset[1] + 1) * 3 + offset[2] + 1
 
+    def blocks_of(step, part):
+        return pl.ds(0, 1) if part == 0 else {-1: pl.ds(1, 1), 0: pl.ds(1, 2), 1: pl.ds(2, 1)}[step]
+
     def near_copy(offset, part):
-        blocks = pl.ds(0, 1) if part == 0 else pl.ds(1, 2)
+        blocks = blocks_of(offset[1], part)
         back = tuple(-step for step in offset)
         start, rows = source_rows[offset[0]]
         goal = target_rows[back[0]][0]
@@ -180,7 +181,7 @@
         )
 
     def near_arrival(offset, part):
-        blocks = pl.ds(0, 1) if part == 0 else pl.ds(1, 2)
+        blocks = blocks_of(-offset[1], part)
         goal, rows = target_rows[offset[0]]
         where = halo.at[offset[1] + 1, offset[2] + 1, blocks, pl.ds(goal, rows), :]
         return pltpu.make_async_remote_copy(
@@ -206,12 +207,12 @@
             total = spread if total is None else [t + s for t, s in zip(total, spread)]
         return total
 
-    pairs = [(k, y) for k in range(3) for y in range(2)]
-    for block, members in ((1, pairs[:4]), (2, pairs[4:])):
-        spread = pack([disp_ref[k, y] for k, y in members])
+    for block in (1, 2):
+        spread = pack([disp_ref[k, block - 1] for k in range(3)])
         for v in range(3):
             packed[v, block] = spread[v]
         halo[1, 1, block, pl.ds(8, cells_x), :] = spread[1]
+    pl.semaphore_wait(barrier, expect)
     for offset in offsets:
 
         @pl.when(inside(offset))
@@ -307,7 +308,15 @@
 
     coarse = centred(0, False)
     deformed = centred(0, True)
-    displacement = [centred(1, False), centred(1, True), centred(2, False)]
+    displacement = []
+    for k in range(3):
+        parts = [
+            pltpu.roll(block, SLOT * ((s - k) % 4), 1) if s != k else block
+            for s, block in enumerate((summed[0][2], summed[1][1], summed[1][2], summed[2][1]))
+        ]
+        displacement.append(
+            jnp.where(slot < 2, jnp.where(slot == 0, parts[0], parts[1]), jnp.where(slot == 2, parts[2], parts[3]))
+        )
     before = jnp.where(slot < 2, summed[0][0], pltpu.roll(summed[1][0], 64, 1))
     after = jnp.where(slot < 2, summed[1][0], pltpu.roll(summed[2][0], 64, 1))
     slopes = [

time: 25.8 us -> 24.3 us (0.942)
  Pallas kernels: 25 us -> 23.5 us
    pallas_call x1, Pallas kernels: 17.7 us -> 16.2 us  [on_device(): pl.pallas_call(functools.partial(exchange, counts), out_shape=(shape(cell...]
where the time goes in v3:
time: 24.3 us; the launch traced here: 24.1 us
  Pallas kernels  23.5 us (97%)
  between operations  0.64 us (3%)
    pallas_call x1, Pallas kernels, on_device(): pl.pallas_call(functools.partial(exchange, counts), out_shape=(shape(cell...  16.2 us
    pallas_call x1, Pallas kernels, on_device(): pl.pallas_call(functools.partial(combine, counts, chunks), out_shape=(sha...  7.25 us

profile of v3, /device:TPU:0, one launch (start us, length us, event | category | flops | bytes accessed | tf_op | source)
XLA Modules:
  0.0 24.1 jit_solution(17697701807987236415)
XLA Ops:
  0.6 16.2 %shard_map.95 = (f32[3,2,16,32]{3,2,1,0:T(8,128)S(1)}, f32[3,4,48,128]{3,2,1,0:T(8,128)S(1)}, bf16[258,16,128]{2,1,0:T(8,128)(2,1)S(1)}, bf16[256,16,128]{2,1,0:...) custom-call(bf16[256,16,128]{2,1,0:T(8,128)(2,1)} %ref_hbm.1, ...), custom_call_target="tpu_custom_call" | custom-call | tf_op jit(solution)/shard_map/pallas_call | solution.py:521
  16.9 7.3 %shard_map.96 = (f32[3,2,16,32]{3,2,1,0:T(8,128)}, bf16[256,16,128]{2,1,0:T(8,128)(2,1)}) custom-call(f32[3,2,16,32]{3,2,1,0:T(8,128)S(1)} %get-tuple-element.10.new_in, f32[3,4,48,128]{3,2,1,0:T(8,128)S(1)} %get-tuple-element.11.lines, bf16[258,16,128]{2,1,0:T(8,128)(2,1)S(1)} %get-tuple-element.12.refs, bf16[256,16,128]{2,1,0:T(8,128)(2,1)S(1)} %get-tuple-element.13.defs, ...), custom_call_target="tpu_custom_call" | custom-call | tf_op jit(solution)/shard_map/pallas_call | solution.py:558
